TPU v7x, 8 devices: a whole 2x2x1 slice. The times are simulated.
8 devices in a mesh: dp: 2 (over z, y), ep: 4 (over x, core).
Axes of the slice: x: 2, y: 2, z: 1, core: 2. Of those that a mesh axis runs over, the one named last changes fastest.
Arguments:
- x: bfloat16 [16384, 768], P(('dp', 'ep'))
- gy: bfloat16 [16384, 768], P(('dp', 'ep'))
- idx: int32 [16384], P(('dp', 'ep'))
- w_gate: bfloat16 [768, 8], replicated
- w_up: bfloat16 [8, 768, 3072], P('ep')
- w_down: bfloat16 [8, 3072, 768], P('ep')
Outputs:
- output 1: bfloat16 [16384, 768], P(('dp', 'ep'))
- output 2: bfloat16 [16384, 768], P(('dp', 'ep'))
- output 3: float32 [8, 768, 3072], P('ep')
- output 4: float32 [8, 3072, 768], P('ep')
- output 5: float32 [768, 8], replicated
All inputs are finite; a program needn't handle non-finite values.
Results may differ from a plain program's by a relative error of at most 0.00593475.
Values are sent between devices in bfloat16 or wider.
A program may use at most 1 GiB of HBM per device.

v0:
```python
import jax
import jax.numpy as jnp
from jax import lax
from jax.sharding import PartitionSpec as P

PAD_FACTOR = 4


def solution(mesh):
    ep_size = mesh.shape['ep']
    tok_spec = P(('dp', 'ep'), None)
    idx_spec = P(('dp', 'ep'))
    rep_spec = P(None, None)
    exp_spec = P('ep', None, None)

    def local_step(x_loc, gy_loc, idx_loc, w_gate, w_up, w_down):
        tok_count, d_model = x_loc.shape
        n_experts = w_gate.shape[1]
        local_experts = w_up.shape[0]
        cap_rows = PAD_FACTOR * tok_count // n_experts
        onehot = idx_loc[:, None] == jnp.arange(n_experts, dtype=jnp.int32)[None, :]
        expert_count = jnp.sum(onehot, axis=0, dtype=jnp.int32)
        sort_order = jnp.argsort(idx_loc, stable=True)
        sorted_pos = jnp.argsort(sort_order)
        expert_start = jnp.cumsum(expert_count) - expert_count
        slot_k = jnp.arange(cap_rows, dtype=jnp.int32)
        slot_valid = slot_k[None, :] < expert_count[:, None]
        src_tok = sort_order[jnp.minimum(expert_start[:, None] + slot_k[None, :], tok_count - 1)]
        slot_tok = idx_loc * cap_rows + sorted_pos - expert_start[idx_loc]

        def dispatch(tok_rows):
            picked = jnp.where(slot_valid[:, :, None], tok_rows[src_tok], jnp.zeros((), tok_rows.dtype))
            picked = picked.reshape(ep_size, local_experts, cap_rows, d_model)
            return lax.all_to_all(picked, 'ep', 0, 0, tiled=True)

        def combine(expert_rows):
            returned = lax.all_to_all(expert_rows, 'ep', 1, 0, tiled=True)
            return returned.reshape(n_experts * cap_rows, d_model)[slot_tok]

        router_logit = jnp.dot(x_loc, w_gate, preferred_element_type=jnp.float32)
        router_prob = jax.nn.softmax(router_logit, axis=-1)
        gate_val = n_experts * jnp.sum(jnp.where(onehot, router_prob, 0.0), axis=1)
        recv_rows = dispatch(x_loc)
        pre_act = jnp.einsum('sekd,edf->eskf', recv_rows, w_up, preferred_element_type=jnp.float32)
        hid_full, gelu_back = jax.vjp(jax.nn.gelu, pre_act)
        hidden = hid_full.astype(jnp.bfloat16)
        expert_out = jnp.einsum('eskf,efd->eskd', hidden, w_down, preferred_element_type=jnp.float32).astype(jnp.bfloat16)
        y_tok = combine(expert_out)
        gy_full = gy_loc.astype(jnp.float32)
        moe_out = (gate_val[:, None] * y_tok.astype(jnp.float32)).astype(jnp.bfloat16)

        dy_tok = (gate_val[:, None] * gy_full).astype(jnp.bfloat16)
        recv_grad = dispatch(dy_tok)
        d_hidden = jnp.einsum('sekd,efd->eskf', recv_grad, w_down, preferred_element_type=jnp.float32)
        d_pre = gelu_back(d_hidden)[0].astype(jnp.bfloat16)
        grad_down = jnp.einsum('eskf,sekd->efd', hidden, recv_grad, preferred_element_type=jnp.float32)
        grad_up = jnp.einsum('sekd,eskf->edf', recv_rows, d_pre, preferred_element_type=jnp.float32)
        d_rows = jnp.einsum('eskf,edf->eskd', d_pre, w_up, preferred_element_type=jnp.float32).astype(jnp.bfloat16)
        dx_expert = combine(d_rows)
        d_gate = jnp.sum(gy_full * y_tok.astype(jnp.float32), axis=1)
        d_logit = ((d_gate * gate_val)[:, None] * (onehot.astype(jnp.float32) - router_prob)).astype(jnp.bfloat16)
        dx_router = jnp.einsum('te,de->td', d_logit, w_gate, preferred_element_type=jnp.float32)
        grad_x = (dx_expert.astype(jnp.float32) + dx_router).astype(jnp.bfloat16)
        grad_gate = jnp.einsum('td,te->de', x_loc, d_logit, preferred_element_type=jnp.float32)
        grad_up = lax.psum(grad_up, 'dp')
        grad_down = lax.psum(grad_down, 'dp')
        grad_gate = lax.psum(grad_gate, ('dp', 'ep'))
        return moe_out, grad_x, grad_up, grad_down, grad_gate

    sharded_fn = jax.shard_map(local_step, mesh=mesh, in_specs=(tok_spec, tok_spec, idx_spec, rep_spec, exp_spec, exp_spec), out_specs=(tok_spec, tok_spec, exp_spec, exp_spec, rep_spec), check_vma=False)
    return sharded_fn
```

profile of v0, /device:TPU:0, one launch (start us, length us, event | category | flops | bytes accessed | tf_op | source)
XLA Modules:
  0.0 1772.1 jit_solution(15650874393636700720)
XLA Ops:
  14.3 45.5 %gather_fusion = s32[8192]{0:T(1024)S(1)} fusion(s32[2048]{0:T(1024)S(1)} %get-tuple-element.7, s32[8192]{0:T(1024)S(1)} %bitcast_clamp_fusion.1), kind=kCustom, calls=%fused_computation | custom fusion | bytes 98304 | tf_op jit(solution)/shard_map/gather | solution.py:28
  60.0 34.4 %gather_fusion.1 = bf16[8192,768]{1,0:T(8,128)(2,1)} fusion(bf16[2048,768]{1,0:T(8,128)(2,1)S(1)} %copy-done, s32[8192]{0:T(1024)S(1)} %bitcast_clamp_fusion), kind=kCustom, calls=%fused_computation.1 | custom fusion | bytes 25198592 | tf_op jit(solution)/shard_map/gather | solution.py:32
  94.5 6.9 broadcast_select_fusion.1
  101.4 143.4 %all_to_all.40 = bf16[4,2,1024,768]{3,2,1,0:T(8,128)(2,1)} all-to-all(bf16[4,2,1024,768]{3,2,1,0:T(8,128)(2,1)S(1)} %broadcast_select_fusion.1), channel_id=1, replica_groups=mesh['dp'=2,'ep'=4] {'ep'}, dimensions={0} | all-to-all | bytes 25165824 | tf_op jit(solution)/shard_map/all_to_all | solution.py:34
  244.8 70.2 %multiply_convert_fusion = (bf16[2,4,1024,3072]{3,2,1,0:T(8,128)(2,1)}, f32[2,4,1024,3072]{3,2,1,0:T(8,128)}) fusion(bf16[2,768,3072]{2,1,0:T(8,128)(2,1)} %param.10, bf16[4,2,1024,768]{3,2,1,0:T(8,128)(2,1)} %all_to_all.40), kind=kOutput, calls=%fused_computation.14 | convolution fusion | flops 38881198080 | bytes 173015040 | tf_op jit(solution)/shard_map/sekd,edf->eskf/dot_general | solution.py:44
  315.0 45.9 %fusion.26 = bf16[2,4,1024,768]{3,2,1,0:T(8,128)(2,1)S(1)} fusion(bf16[2,4,1024,3072]{3,2,1,0:T(8,128)(2,1)} %get-tuple-element.22, bf16[2,3072,768]{2,1,0:T(8,128)(2,1)} %param.11), kind=kOutput, calls=%fused_computation.35 | convolution fusion | flops 38660997120 | bytes 72351744 | tf_op jit(solution)/shard_map/eskf,efd->eskd/dot_general | solution.py:47
  365.9 6.5 all-to-all-start.1
  385.8 124.4 %all-to-all-done.1 = bf16[2,4,1024,768]{3,2,0,1:T(8,128)(2,1)} async-done(((bf16[2,4,1024,768]{3,2,0,1:T(8,128)(2,1)}), bf16[2,4,1024,768]{3,2,0,1:T(8,128)(2,1)}, u32[]{:S(2)}, u32[]{:S(2)}) %all-to-all-start.1) | async-done | bytes 12582944 | tf_op jit(solution)/shard_map/all_to_all | solution.py:37
  510.2 16.3 gather_fusion.2
  526.4 6.0 fusion.34
  532.4 39.3 %gather_fusion.3 = bf16[8192,768]{1,0:T(8,128)(2,1)} fusion(bf16[2048,768]{1,0:T(8,128)(2,1)} %get-tuple-element.12, s32[8192]{0:T(1024)S(1)} %copy-done.8), kind=kCustom, calls=%fused_computation.3 | custom fusion | bytes 25198592 | tf_op jit(solution)/shard_map/gather | solution.py:32
  571.8 6.9 broadcast_select_fusion
  578.7 142.2 %all_to_all.41 = bf16[4,2,1024,768]{3,2,1,0:T(8,128)(2,1)} all-to-all(bf16[4,2,1024,768]{3,2,1,0:T(8,128)(2,1)S(1)} %broadcast_select_fusion), channel_id=1, replica_groups=mesh['dp'=2,'ep'=4] {'ep'}, dimensions={0} | all-to-all | bytes 25165824 | tf_op jit(solution)/shard_map/all_to_all | solution.py:34
  720.8 48.5 %fusion.20 = f32[2,3072,768]{2,1,0:T(8,128)} fusion(bf16[2,4,1024,3072]{3,2,1,0:T(8,128)(2,1)} %get-tuple-element.22, bf16[4,2,1024,768]{3,2,1,0:T(8,128)(2,1)} %all_to_all.41), kind=kOutput, calls=%fused_computation.30 | convolution fusion | flops 38654705664 | bytes 81788928 | tf_op jit(solution)/shard_map/eskf,sekd->efd/dot_general | solution.py:56
  769.4 98.3 %fusion.6 = bf16[2,4,1024,3072]{3,2,1,0:T(8,128)(2,1)} fusion(f32[2,4,1024,3072]{3,2,1,0:T(8,128)} %get-tuple-element.23, bf16[4,2,1024,768]{3,2,1,0:T(8,128)(2,1)} %all_to_all.41, bf16[2,3072,768]{2,1,0:T(8,128)(2,1)} %param.11), kind=kOutput, calls=%fused_computation.13 | convolution fusion | flops 39158022144 | bytes 173015040 | tf_op jit(solution)/shard_map/sekd,efd->eskf/dot_general | solution.py:54
  867.7 47.8 %fusion.23 = f32[2,768,3072]{2,1,0:T(8,128)} fusion(bf16[4,2,1024,768]{3,2,1,0:T(8,128)(2,1)} %all_to_all.40, bf16[2,4,1024,3072]{3,2,1,0:T(8,128)(2,1)} %fusion.6), kind=kOutput, calls=%fused_computation.31 | convolution fusion | flops 38654705664 | bytes 81788928 | tf_op jit(solution)/shard_map/sekd,eskf->edf/dot_general | solution.py:57
  915.5 47.3 %fusion.29 = bf16[2,4,1024,768]{3,2,1,0:T(8,128)(2,1)} fusion(bf16[2,4,1024,3072]{3,2,1,0:T(8,128)(2,1)} %fusion.6, bf16[2,768,3072]{2,1,0:T(8,128)(2,1)} %param.10), kind=kOutput, calls=%fused_computation.36 | convolution fusion | flops 38660997120 | bytes 72351744 | tf_op jit(solution)/shard_map/eskf,edf->eskd/dot_general | solution.py:58
  962.9 10.7 copy.24
  973.6 6.7 all-to-all-start.3
  980.9 156.5 %psum.23 = f32[768,8]{0,1:T(8,128)} all-reduce(f32[768,8]{0,1:T(8,128)S(1)} %convolution_bitcast_fusion), channel_id=1, replica_groups=mesh['dp'=2,'ep'=4] {'dp','ep'}, use_global_device_ids=true, to_apply=%region_10.11 | all-reduce | flops 6144 | bytes 49152 | tf_op jit(solution)/shard_map/psum | solution.py:67
  1137.4 16.3 gather_fusion.4
  1158.3 581.4 %all-reduce.3.cloned.1.call-done = (f32[2,768,3072]{2,1,0:T(8,128)}, f32[2,3072,768]{2,1,0:T(8,128)}) async-done(((f32[2,768,3072]{2,1,0:T(8,128)}, f32[2,3072,768]{2,1,0:T(8,128)}), (f32[2,768,3072]{2,1,0:T(8,128)}, f32[2,3072,768]{2,1,0:T(8,128)})) %all-reduce.3.cloned.1.call-update) | async-done | bytes 37748752 | tf_op jit(solution)/shard_map/psum | solution.py:65
  1739.7 14.9 copy.54
  1758.1 6.8 copy.55
  (86 shorter events, 34.3 us)
Async XLA Ops:
  7.2 52.8 %copy-start = (bf16[2048,768]{1,0:T(8,128)(2,1)S(1)}, bf16[2048,768]{1,0:T(8,128)(2,1)}, u32[]{:S(2)}) copy-start(bf16[2048,768]{1,0:T(8,128)(2,1)} %param.6) | copy-start | bytes 9437188
  14.2 45.6 %copy-start.1 = (s32[2048]{0:T(1024)}, s32[2048]{0:T(1024)S(1)}, u32[]{:S(2)}) copy-start(s32[2048]{0:T(1024)S(1)} %get-tuple-element.7) | copy-start | bytes 24580
  59.9 34.6 %copy-start.7 = (s32[8192]{0:T(1024)}, s32[8192]{0:T(1024)S(1)}, u32[]{:S(2)}) copy-start(s32[8192]{0:T(1024)S(1)} %bitcast_clamp_fusion) | copy-start | bytes 98308
  60.0 34.5 %copy-start.11 = (pred[4,2,1024]{2,1,0:T(4,128)(4,1)}, pred[4,2,1024]{2,1,0:T(4,128)(4,1)S(1)}, u32[]{:S(2)}) copy-start(pred[4,2,1024]{2,1,0:T(4,128)(4,1)S(1)} %iota_compare_fusion.1) | copy-start | bytes 24580
  365.9 7.1 copy-start.2
  365.9 12.2 copy-start.22
  365.9 12.8 copy-start.19
  365.9 14.3 copy-start.5
  365.9 144.2 %all-to-all-start.1 = ((bf16[2,4,1024,768]{3,2,0,1:T(8,128)(2,1)}), bf16[2,4,1024,768]{3,2,0,1:T(8,128)(2,1)}, u32[]{:S(2)}, u32[]{:S(2)}) async-start(bf16[2,4,1024,768]{3,2,0,1:T(8,128)(2,1)} %copy.22), calls=%async_computation.1 | async-start | bytes 25165824 | tf_op jit(solution)/shard_map/all_to_all | solution.py:37
  372.4 1367.2 %all-reduce.3.cloned.1.call-start = ((), (), s32[]{:S(2)}) async-start(), calls=%async_computation.4 | async-start | bytes 75497472 | tf_op jit(solution)/shard_map/psum | solution.py:65
  385.7 124.4 %copy-start.17 = (s32[2048]{0:T(1024)}, s32[2048]{0:T(1024)S(1)}, u32[]{:S(2)}) copy-start(s32[2048]{0:T(1024)S(1)} %fusion.39) | copy-start | bytes 24580
  532.4 39.4 %copy-start.12 = (pred[4,2,1024]{2,1,0:T(4,128)(4,1)S(1)}, pred[4,2,1024]{2,1,0:T(4,128)(4,1)}, u32[]{:S(2)}) copy-start(pred[4,2,1024]{2,1,0:T(4,128)(4,1)} %copy-done.11) | copy-start | bytes 24580
  973.5 6.8 copy-start.4
  973.5 6.8 copy-start.6
  973.5 6.8 copy-start.10
  973.5 6.8 copy-start.14
  973.6 163.8 %copy-start.18 = (s32[2048]{0:T(1024)S(1)}, s32[2048]{0:T(1024)}, u32[]{:S(2)}) copy-start(s32[2048]{0:T(1024)} %copy-done.17) | copy-start | bytes 24580
  973.6 163.8 %all-to-all-start.3 = ((bf16[2,4,1024,768]{3,2,0,1:T(8,128)(2,1)}), bf16[2,4,1024,768]{3,2,0,1:T(8,128)(2,1)}, u32[]{:S(2)}, u32[]{:S(2)}) async-start(bf16[2,4,1024,768]{3,2,0,1:T(8,128)(2,1)} %copy.24), calls=%async_computation.3 | async-start | bytes 25165824 | tf_op jit(solution)/shard_map/all_to_all | solution.py:37
  1137.4 16.3 copy-start.20
  1739.6 14.9 slice-start
  1739.7 14.9 slice-start.1
  1739.7 16.6 slice-start.2
  1739.7 17.8 %slice-start.3 = ((s8[18874368]{0:T(1024)(128)(4,1)}), s8[4194304]{0:T(1024)(128)(4,1)S(1)}, s32[]{:S(2)}) async-start(s8[18874368]{0:T(1024)(128)(4,1)} %bitcast.70), calls=%async_computation.8 | async-start | bytes 8388608
  1739.7 18.4 %slice-start.4 = ((s8[18874368]{0:T(1024)(128)(4,1)}), s8[2097152]{0:T(1024)(128)(4,1)S(1)}, s32[]{:S(2)}) async-start(s8[18874368]{0:T(1024)(128)(4,1)} %bitcast.70), calls=%async_computation.9 | async-start | bytes 4194304
  (8 other events, 27.8 us)
Sparse Core Ops, SparseCore 0:
  915.7 823.9 all-reduce.2
where the time goes:
time: 1780 us; the launch traced here: 1770 us
  waiting for transfers between devices  706 us (40%)
  blocking collectives  442 us (25%)
  matrix products  364 us (20%)
  local copies, waits for them, and re-layouts  195 us (11%)
  other arithmetic  36.8 us (2%)
    psum x1, waiting for transfers between devices, local_step(): grad_up = lax.psum(grad_up, 'dp')  581 us
    all_to_all x2, blocking collectives, dispatch(): return lax.all_to_all(picked, 'ep', 0, 0, tiled=True)  286 us
    psum x1, blocking collectives, local_step(): grad_gate = lax.psum(grad_gate, ('dp', 'ep'))  156 us
    all_to_all x2, waiting for transfers between devices, combine(): returned = lax.all_to_all(expert_rows, 'ep', 1, 0, tiled=True)  124 us
    dot_general x1, matrix products, local_step(): jnp.einsum('sekd,efd->eskf', recv_grad, w_down, preferred_element_type=jn...  98.3 us
    gather x2, local copies, waits for them, and re-layouts, dispatch(): tok_rows[src_tok]  73.8 us
    dot_general x1, matrix products, local_step(): jnp.einsum('sekd,edf->eskf', recv_rows, w_up, preferred_element_type=jnp....  70.2 us
    dot_general x1, matrix products, local_step(): jnp.einsum('eskf,sekd->efd', hidden, recv_grad, preferred_element_type=jn...  48.5 us
  transfers between devices with their start and end apart: 3, of which 2 were waited for; matrix products, arithmetic and copies ran while one was open for 5% of the time, Pallas kernels for 0%

commit v1 on v0

v1 whole, which is shorter than its diff:
```python
import functools
import jax
import jax.numpy as jnp
from jax import lax
from jax.experimental import pallas as pl
from jax.experimental.pallas import tpu as pltpu
from jax.sharding import PartitionSpec as P


BLK = 16
N_COL = 2
FC = 512
F32 = jnp.float32
BF16 = jnp.bfloat16
GELU_C = 0.7978845608028654
GELU_K = 0.044715
VMEM_LIMIT = 66 * 1000 * 1000


def _any():
    return pl.BlockSpec(memory_space=pl.ANY)


def _smem():
    return pl.BlockSpec(memory_space=pltpu.SMEM)


def _sort_x_kernel(n_exp, rows_buf, idx_ref, x_ref, xs_ref, pos_ref, meta_ref, pos_scr):
    tok = idx_ref.shape[1]
    rows = xs_ref.shape[0]
    step = pl.program_id(0)
    grp = n_exp // N_COL

    @pl.when(step == 0)
    def _():
        col = lax.axis_index('ep') // 2
        exp_iota = lax.broadcasted_iota(jnp.int32, (16, 256), 0)
        tri = (lax.broadcasted_iota(jnp.int32, (256, 256), 0)
               <= lax.broadcasted_iota(jnp.int32, (256, 256), 1)).astype(F32).astype(BF16)
        nchunk = tok // 256
        prefix = []
        carry = jnp.zeros((16, 1), F32)
        for c in range(nchunk):
            oh = (idx_ref[:, c * 256:(c + 1) * 256] == exp_iota).astype(F32).astype(BF16)
            pre = jnp.dot(oh, tri, preferred_element_type=F32)
            prefix.append(pre + (carry - 1.0))
            carry = carry + pre[:, 255:256]
        cnt = carry.astype(jnp.int32)
        nblk = (cnt + (BLK - 1)) >> 4
        start = jnp.zeros((16, 1), jnp.int32)
        iota_col = lax.broadcasted_iota(jnp.int32, (16, 1), 0)
        for g in range(N_COL):
            pre_e = jnp.zeros((1, 1), jnp.int32)
            tot = jnp.zeros((1, 1), jnp.int32)
            for e in range(g * grp, (g + 1) * grp):
                tot = tot + nblk[e:e + 1, :]
            local = (col == g)
            base = jnp.where(local, rows_buf // BLK - tot, 0)
            for e in range(g * grp, (g + 1) * grp):
                start = jnp.where(iota_col == e, base + pre_e, start)
                pre_e = pre_e + nblk[e:e + 1, :]
        lane = lax.broadcasted_iota(jnp.int32, (16, 128), 1)
        meta_ref[...] = jnp.where(lane == 0, start, jnp.where(lane == 1, nblk, 0))
        startf = (start * BLK).astype(F32)
        for c in range(nchunk):
            oh = idx_ref[:, c * 256:(c + 1) * 256] == exp_iota
            p = jnp.sum(jnp.where(oh, prefix[c] + startf, 0.0), axis=0, keepdims=True)
            pos_scr[:, c * 256:(c + 1) * 256] = p.astype(jnp.int32)
        pos_ref[...] = pos_scr[...]

    dst = lax.broadcasted_iota(jnp.int32, (rows, tok), 0) + step * rows
    perm = (dst == pos_scr[...]).astype(F32).astype(BF16)
    xs_ref[...] = jnp.dot(perm, x_ref[...], preferred_element_type=F32).astype(BF16)


def _sort_dy_kernel(n_exp, pos_ref, idxc_ref, x_ref, gy_ref, wg_ref, dys_ref, dy_scr):
    tok = pos_ref.shape[1]
    rows = dys_ref.shape[0]
    step = pl.program_id(0)

    @pl.when(step == 0)
    def _():
        for c in range(tok // 256):
            sl = slice(c * 256, (c + 1) * 256)
            _, _, gate = _router(n_exp, x_ref[sl, :], idxc_ref[sl, :], wg_ref[...])
            dy_scr[sl, :] = (gate * gy_ref[sl, :].astype(F32)).astype(BF16)

    dst = lax.broadcasted_iota(jnp.int32, (rows, tok), 0) + step * rows
    perm = (dst == pos_ref[...]).astype(F32).astype(BF16)
    dys_ref[...] = jnp.dot(perm, dy_scr[...], preferred_element_type=F32).astype(BF16)


def _router(n_exp, x, idx_col, wg):
    lane = lax.broadcasted_iota(jnp.int32, (x.shape[0], wg.shape[1]), 1)
    z = jnp.dot(x, wg, preferred_element_type=F32)
    z = jnp.where(lane < n_exp, z, -jnp.inf)
    ez = jnp.exp(z - jnp.max(z, axis=1, keepdims=True))
    prob = ez / jnp.sum(ez, axis=1, keepdims=True)
    onehot = lane == idx_col
    gate = n_exp * jnp.sum(jnp.where(onehot, prob, 0.0), axis=1, keepdims=True)
    return prob, onehot, gate


def _bits(maxblk):
    b = 1
    while b * 2 <= maxblk:
        b *= 2
    out = []
    while b >= 1:
        out.append(b)
        b //= 2
    return out


def _wait_blocks(n, maxblk, src, dst, sem):
    for b in _bits(maxblk):
        @pl.when((n & b) != 0)
        def _(b=b):
            pltpu.make_async_copy(src.at[pl.ds(0, b * BLK), :], dst.at[pl.ds(0, b * BLK), :], sem).wait()


def _moe_kernel(cfg, *refs):
    n_src, own, acc_in, n_loc, dp_flip, ep_flips, seg_max = cfg
    refs = list(refs)
    meta = refs.pop(0)
    xs = [refs.pop(0) for _ in range(n_src)]
    dys = [refs.pop(0) for _ in range(n_src)]
    w1 = refs.pop(0)
    w2 = refs.pop(0)
    if acc_in:
        g1i = refs.pop(0)
        g2i = refs.pop(0)
    g1o = refs.pop(0)
    g2o = refs.pop(0)
    ys, dxs = [], []
    if own:
        ys = [refs.pop(0) for _ in range(n_src)]
        dxs = [refs.pop(0) for _ in range(n_src)]
    xb = refs.pop(0)
    db = refs.pop(0)
    if own:
        ya = refs.pop(0)
        da_acc = refs.pop(0)
    w1c = refs.pop(0)
    w2c = refs.pop(0)
    a1 = refs.pop(0)
    a2 = refs.pop(0)
    in_sem = refs.pop(0)
    out_sem = refs.pop(0)
    w_sem = refs.pop(0)
    ld_sem = refs.pop(0)
    st_sem = refs.pop(0)

    d_model = w1.shape[1]
    d_ff = w1.shape[2]
    nf = d_ff // FC
    nq = n_loc * nf
    dp = lax.axis_index('dp')
    ep = lax.axis_index('ep')
    n_exp = 4 * n_loc
    seg_bits = _bits(seg_max)

    def seg(e, s):
        sdp = (1 - dp) if dp_flip else dp
        sep = ep ^ ep_flips[s]
        base = ((sdp * 4 + sep) * n_exp + ep * n_loc + e) * 2
        return meta[base], meta[base + 1]

    segs = [[seg(e, s) for s in range(n_src)] for e in range(n_loc)]
    tot = []
    for e in range(n_loc):
        t = segs[e][0][1]
        for s in range(1, n_src):
            t = t + segs[e][s][1]
        tot.append(t)

    def pick(vals, e):
        r = vals[0]
        for i in range(1, n_loc):
            r = jnp.where(e == i, vals[i], r)
        return r

    def seg_loop(e, fn):
        at = jnp.int32(0)
        for s in range(n_src):
            first, num = segs[e][s]
            for b in seg_bits:
                off = num - (num & (2 * b - 1))

                @pl.when((num & b) != 0)
                def _(s=s, b=b, off=off, first=first, at=at):
                    hb = pl.multiple_of((first + off) * BLK, BLK)
                    vb = pl.multiple_of((at + off) * BLK, BLK)
                    fn(s, pl.ds(hb, b * BLK), pl.ds(vb, b * BLK))
            at = at + num

    def w_copies(q):
        e, f, sl = q // nf, q % nf, q % 2
        fo = pl.multiple_of(f * FC, FC)
        return (pltpu.make_async_copy(w1.at[e, :, pl.ds(fo, FC)], w1c.at[sl], w_sem.at[sl, 0]),
                pltpu.make_async_copy(w2.at[e, pl.ds(fo, FC), :], w2c.at[sl], w_sem.at[sl, 1]))

    def ld_copies(q):
        e, f, sl = q // nf, q % nf, q % 3
        fo = pl.multiple_of(f * FC, FC)
        return (pltpu.make_async_copy(g1i.at[e, :, pl.ds(fo, FC)], a1.at[sl], ld_sem.at[sl, 0]),
                pltpu.make_async_copy(g2i.at[e, pl.ds(fo, FC), :], a2.at[sl], ld_sem.at[sl, 1]))

    def st_copies(q):
        e, f, sl = q // nf, q % nf, q % 3
        fo = pl.multiple_of(f * FC, FC)
        return (pltpu.make_async_copy(a1.at[sl], g1o.at[e, :, pl.ds(fo, FC)], st_sem.at[sl, 0]),
                pltpu.make_async_copy(a2.at[sl], g2o.at[e, pl.ds(fo, FC), :], st_sem.at[sl, 1]))

    def start(cs):
        for c in cs:
            c.start()

    def wait(cs):
        for c in cs:
            c.wait()

    start(w_copies(0))
    if acc_in:
        start(ld_copies(0))
    for e in range(n_loc):
        def load(s, hs, vs, e=e):
            pltpu.make_async_copy(xs[s].at[hs, :], xb.at[e, vs, :], in_sem.at[e, 0]).start()
            pltpu.make_async_copy(dys[s].at[hs, :], db.at[e, vs, :], in_sem.at[e, 1]).start()

        seg_loop(e, load)

    def tile(e, r, m, ws, sl):
        r = pl.multiple_of(r, 256)
        x = xb[e, pl.ds(r, m), :]
        dy = db[e, pl.ds(r, m), :]
        a = jnp.dot(x, w1c[ws], preferred_element_type=F32)
        dh = lax.dot_general(dy, w2c[ws], (((1,), (1,)), ((), ())), preferred_element_type=F32)
        a_sq = a * a
        t = jnp.tanh(a * (GELU_C + (GELU_C * GELU_K) * a_sq))
        p = 0.5 + 0.5 * t
        hf = a * p
        gp = p + hf * (1.0 - p) * (2.0 * GELU_C + (6.0 * GELU_C * GELU_K) * a_sq)
        h = hf.astype(BF16)
        da = (gp * dh).astype(BF16)
        if own:
            ya[pl.ds(r, m), :] += jnp.dot(h, w2c[ws], preferred_element_type=F32)
            da_acc[pl.ds(r, m), :] += lax.dot_general(da, w1c[ws], (((1,), (1,)), ((), ())),
                                                      preferred_element_type=F32)
        a2[sl] += lax.dot_general(h, dy, (((0,), (0,)), ((), ())), preferred_element_type=F32)
        a1[sl] += lax.dot_general(x, da, (((0,), (0,)), ((), ())), preferred_element_type=F32)

    def q_step(q, _):
        e, f = q // nf, q % nf
        ws, sl = q % 2, q % 3
        total = pick(tot, e)
        n256 = (total + 15) >> 4

        @pl.when(f == 0)
        def _():
            for s in range(n_src):
                num = pick([segs[i][s][1] for i in range(n_loc)], e)
                _wait_blocks(num, seg_max, xs[0], xb.at[e], in_sem.at[e, 0])
                _wait_blocks(num, seg_max, dys[0], db.at[e], in_sem.at[e, 1])

            def zero_rows(b, _):
                rs = pl.ds(pl.multiple_of(b * BLK, BLK), BLK)
                xb[e, rs, :] = jnp.zeros((BLK, d_model), BF16)
                db[e, rs, :] = jnp.zeros((BLK, d_model), BF16)
                return 0

            lax.fori_loop(total, n256 * 16, zero_rows, 0)
            if own:
                def zero_acc(b, _):
                    rs = pl.ds(pl.multiple_of(b * 256, 256), 256)
                    ya[rs, :] = jnp.zeros((256, d_model), F32)
                    da_acc[rs, :] = jnp.zeros((256, d_model), F32)
                    return 0

                lax.fori_loop(0, n256, zero_acc, 0)

        if acc_in:
            @pl.when(q + 1 < nq)
            def _():
                @pl.when(q >= 2)
                def _():
                    wait(st_copies(q - 2))

                start(ld_copies(q + 1))

            wait(ld_copies(q))
        else:
            @pl.when(q >= 3)
            def _():
                wait(st_copies(q - 3))

            a1[sl] = jnp.zeros(a1.shape[1:], F32)
            a2[sl] = jnp.zeros(a2.shape[1:], F32)
        wait(w_copies(q))

        @pl.when(q + 1 < nq)
        def _():
            start(w_copies(q + 1))

        n512 = n256 >> 1
        lax.fori_loop(0, n512, lambda i, _: (tile(e, i * 512, 512, ws, sl), 0)[1], 0)

        @pl.when((n256 & 1) == 1)
        def _():
            tile(e, n512 * 512, 256, ws, sl)

        start(st_copies(q))

        if own:
            @pl.when(f == nf - 1)
            def _():
                def cast(b, _):
                    rs = pl.ds(pl.multiple_of(b * 256, 256), 256)
                    xb[e, rs, :] = ya[rs, :].astype(BF16)
                    db[e, rs, :] = da_acc[rs, :].astype(BF16)
                    return 0

                lax.fori_loop(0, n256, cast, 0)
                for i in range(n_loc):
                    @pl.when(e == i)
                    def _(i=i):
                        def put(s, hs, vs):
                            pltpu.make_async_copy(xb.at[i, vs, :], ys[s].at[hs, :], out_sem.at[i, 0]).start()
                            pltpu.make_async_copy(db.at[i, vs, :], dxs[s].at[hs, :], out_sem.at[i, 1]).start()

                        seg_loop(i, put)
        return 0

    lax.fori_loop(0, nq, q_step, 0)
    for q in range(nq - 3, nq):
        wait(st_copies(q))
    if own:
        for i in range(n_loc):
            for s in range(n_src):
                _wait_blocks(segs[i][s][1], seg_max, xb.at[i], ys[0], out_sem.at[i, 0])
                _wait_blocks(segs[i][s][1], seg_max, db.at[i], dxs[0], out_sem.at[i, 1])


def _moe_call(meta, xs, dys, w1, w2, own, acc, dp_flip, ep_flips, seg_max, flops):
    n_src = len(xs)
    n_loc, d_model, _ = w1.shape
    cap = n_src * seg_max * BLK
    g_shapes = [jax.ShapeDtypeStruct(w1.shape, F32), jax.ShapeDtypeStruct(w2.shape, F32)]
    outs = list(g_shapes)
    if own:
        outs += [jax.ShapeDtypeStruct(a.shape, BF16) for a in xs] * 2
    scratch = [pltpu.VMEM((n_loc, cap, d_model), BF16)] * 2
    if own:
        scratch += [pltpu.VMEM((cap, d_model), F32)] * 2
    scratch += [
        pltpu.VMEM((2, d_model, FC), BF16), pltpu.VMEM((2, FC, d_model), BF16),
        pltpu.VMEM((3, d_model, FC), F32), pltpu.VMEM((3, FC, d_model), F32),
        pltpu.SemaphoreType.DMA((n_loc, 2)), pltpu.SemaphoreType.DMA((n_loc, 2)),
        pltpu.SemaphoreType.DMA((2, 2)), pltpu.SemaphoreType.DMA((3, 2)), pltpu.SemaphoreType.DMA((3, 2)),
    ]
    args = [meta, *xs, *dys, w1, w2]
    aliases = {}
    if acc is not None:
        aliases = {len(args): 0, len(args) + 1: 1}
        args += list(acc)
    cfg = (n_src, own, acc is not None, n_loc, dp_flip, ep_flips, seg_max)
    return pl.pallas_call(
        functools.partial(_moe_kernel, cfg),
        out_shape=outs,
        in_specs=[_smem()] + [_any()] * (len(args) - 1),
        out_specs=[_any()] * len(outs),
        scratch_shapes=scratch,
        input_output_aliases=aliases,
        compiler_params=pltpu.CompilerParams(vmem_limit_bytes=VMEM_LIMIT),
        cost_estimate=pl.CostEstimate(flops=flops, bytes_accessed=60_000_000, transcendentals=0),
    )(*args)


def _merge(bounds, far_ref, mine_ref, pair_ref, dst_ref):
    rows = dst_ref.shape[0]
    pre_end, suf_start, split, mine_first = bounds[0], bounds[1], bounds[2], bounds[3]
    step = 272
    for c in range(rows // step):
        row = lax.broadcasted_iota(jnp.int32, (step, 1), 0) + c * step
        sl = slice(c * step, (c + 1) * step)
        first = row < split
        take_mine = first == (mine_first == 1)
        loc = jnp.where(take_mine, mine_ref[sl, :].astype(F32), pair_ref[sl, :].astype(F32))
        far = far_ref[sl, :].astype(F32)
        v = jnp.where(row < pre_end, far, jnp.where(row >= suf_start, loc, 0.0))
        dst_ref[sl, :] = v.astype(BF16)


def _fin_y_kernel(n_exp, bounds, far_ref, mine_ref, pair_ref, posc_ref, idxc_ref, x_ref, gy_ref, wg_ref,
                  out_ref, dz_ref, dwg_ref, y_scr):
    step = pl.program_id(0)

    @pl.when(step == 0)
    def _():
        _merge(bounds, far_ref, mine_ref, pair_ref, y_scr)
        dwg_ref[...] = jnp.zeros_like(dwg_ref)

    m = posc_ref.shape[0]
    sel = (lax.broadcasted_iota(jnp.int32, (m, y_scr.shape[0]), 1) == posc_ref[...]).astype(F32).astype(BF16)
    y = jnp.dot(sel, y_scr[...], preferred_element_type=F32)
    prob, onehot, gate = _router(n_exp, x_ref[...], idxc_ref[...], wg_ref[...])
    out_ref[...] = (gate * y).astype(BF16)
    d_gate = jnp.sum(gy_ref[...].astype(F32) * y, axis=1, keepdims=True)
    dz = ((d_gate * gate) * (onehot.astype(F32) - prob)).astype(BF16)
    dz_ref[...] = dz
    dwg_ref[...] += lax.dot_general(x_ref[...], dz, (((0,), (0,)), ((), ())), preferred_element_type=F32)


def _fin_dx_kernel(bounds, far_ref, mine_ref, pair_ref, posc_ref, dz_ref, wg_ref, dx_ref, scr):
    step = pl.program_id(0)

    @pl.when(step == 0)
    def _():
        _merge(bounds, far_ref, mine_ref, pair_ref, scr)

    m = posc_ref.shape[0]
    sel = (lax.broadcasted_iota(jnp.int32, (m, scr.shape[0]), 1) == posc_ref[...]).astype(F32).astype(BF16)
    dxe = jnp.dot(sel, scr[...], preferred_element_type=F32)
    dxr = lax.dot_general(dz_ref[...], wg_ref[...], (((1,), (1,)), ((), ())), preferred_element_type=F32)
    dx_ref[...] = (dxe + dxr).astype(BF16)


def solution(mesh):
    tok_spec = P(('dp', 'ep'), None)
    idx_spec = P(('dp', 'ep'))
    rep_spec = P(None, None)
    exp_spec = P('ep', None, None)
    ep_size = mesh.shape['ep']
    dp_size = mesh.shape['dp']
    n_dev = ep_size * dp_size

    def local_step(x, gy, idx, w_gate, w_up, w_down):
        tok, d_model = x.shape
        n_exp = w_gate.shape[1]
        seg_max = (tok // 2) // BLK
        rows_buf = tok + 128
        ep = lax.axis_index('ep')
        dp = lax.axis_index('dp')
        col = ep // 2
        vm = pltpu.CompilerParams(vmem_limit_bytes=VMEM_LIMIT)
        wg_pad = jnp.pad(w_gate, ((0, 0), (0, 128 - n_exp)))
        idx_row = idx.reshape(1, tok)
        idx_col = idx.reshape(tok, 1)

        def whole(shape):
            return pl.BlockSpec(shape, lambda i: (0,) * len(shape))

        def const_smem():
            return pl.BlockSpec(memory_space=pltpu.SMEM)

        st = rows_buf // 4
        xs, pos, meta = pl.pallas_call(
            functools.partial(_sort_x_kernel, n_exp, rows_buf),
            grid=(4,),
            out_shape=[jax.ShapeDtypeStruct((rows_buf, d_model), BF16),
                       jax.ShapeDtypeStruct((1, tok), jnp.int32),
                       jax.ShapeDtypeStruct((16, 128), jnp.int32)],
            in_specs=[whole((1, tok)), whole((tok, d_model))],
            out_specs=[pl.BlockSpec((st, d_model), lambda i: (i, 0)), whole((1, tok)), whole((16, 128))],
            scratch_shapes=[pltpu.VMEM((1, tok), jnp.int32)],
            compiler_params=vm,
            cost_estimate=pl.CostEstimate(flops=7_000_000_000, bytes_accessed=8_000_000, transcendentals=0),
            name='sort_x',
        )(idx_row, x)
        dys = pl.pallas_call(
            functools.partial(_sort_dy_kernel, n_exp),
            grid=(4,),
            out_shape=jax.ShapeDtypeStruct((rows_buf, d_model), BF16),
            in_specs=[whole((1, tok)), whole((tok, 1)), whole((tok, d_model)), whole((tok, d_model)),
                      whole((d_model, 128))],
            out_specs=pl.BlockSpec((st, d_model), lambda i: (i, 0)),
            scratch_shapes=[pltpu.VMEM((tok, d_model), BF16)],
            compiler_params=vm,
            cost_estimate=pl.CostEstimate(flops=8_000_000_000, bytes_accessed=12_000_000, transcendentals=0),
            name='sort_dy',
        )(pos, idx_col, x, gy, wg_pad)

        meta_loc = meta[:n_exp, :2].reshape(1, n_exp * 2)
        meta_all = lax.all_gather(meta_loc, ('dp', 'ep'), axis=0, tiled=True)
        meta_flat = meta_all.reshape(n_dev * n_exp * 2)

        def pair(a):
            return lax.ppermute(a, 'ep', [(i, i ^ 1) for i in range(ep_size)])

        def cross_x(a):
            return lax.ppermute(a, 'ep', [(i, i ^ 2) for i in range(ep_size)])

        def cross_y(a):
            return lax.ppermute(a, 'dp', [(i, 1 - i) for i in range(dp_size)])

        def moe(*args):
            return _moe_call(meta_flat, *args)

        xs_d = pair(xs)
        xs_x = cross_x(xs)
        xs_y = cross_y(xs)
        dys_d = pair(dys)
        dys_x = cross_x(dys)
        dys_y = cross_y(dys)

        g1, g2, y_0, y_d, dx_0, dx_d = moe(
            [xs, xs_d], [dys, dys_d], w_up, w_down, True, None, False, (0, 1), seg_max, 45_000_000_000)
        xs_xd = pair(xs_x)
        dys_xd = pair(dys_x)
        xs_g = cross_y(xs_x)
        dys_g = cross_y(dys_x)
        xs_yd = pair(xs_y)
        dys_yd = pair(dys_y)
        y_dr = pair(y_d)
        dx_dr = pair(dx_d)
        g1, g2, y_x, y_xd, dx_x, dx_xd = moe(
            [xs_x, xs_xd], [dys_x, dys_xd], w_up, w_down, True, (g1, g2), False, (2, 3), seg_max,
            45_000_000_000)

        meta_t = meta_all.reshape(dp_size, ep_size, n_exp, 2)
        grp = n_exp // N_COL
        m_far = lax.dynamic_slice(meta_t, (dp, ep ^ 2, grp * col + grp // 2, 0), (1, 1, 1, 1)).reshape(())
        row = lax.broadcasted_iota(jnp.int32, (rows_buf, 1), 0)
        take = (row < m_far * BLK) == ((ep % 2) == 0)
        y_m = jnp.where(take, y_x, pair(y_xd))
        dx_m = jnp.where(take, dx_x, pair(dx_xd))
        y_ret = cross_x(y_m)
        dx_ret = cross_x(dx_m)

        g1, g2 = moe(
            [xs_y, xs_yd], [dys_y, dys_yd], w_up, w_down, False, (g1, g2), True, (0, 1), seg_max,
            30_000_000_000)
        xs_gd = pair(xs_g)
        dys_gd = pair(dys_g)
        g1, g2 = moe(
            [xs_g, xs_gd], [dys_g, dys_gd], w_up, w_down, False, (g1, g2), True, (2, 3), seg_max,
            30_000_000_000)

        mine = lax.dynamic_slice(meta_t, (dp, ep, 0, 0), (1, 1, n_exp, 2)).reshape(n_exp, 2)
        far_last = lax.dynamic_slice(mine, (grp * (1 - col) + grp - 1, 0), (1, 2)).reshape(2)
        near = lax.dynamic_slice(mine, (grp * col, 0), (grp, 2))
        b_iota = lax.broadcasted_iota(jnp.int32, (4,), 0)
        bounds = jnp.where(b_iota == 0, (far_last[0] + far_last[1]) * BLK,
                           jnp.where(b_iota == 1, near[0, 0] * BLK,
                                     jnp.where(b_iota == 2, near[grp // 2, 0] * BLK, 1 - ep % 2)))
        pos_col = pos.reshape(tok, 1)
        tm = 256

        def rows_spec(width):
            return pl.BlockSpec((tm, width), lambda i: (i, 0))

        moe_out, dz, dwg = pl.pallas_call(
            functools.partial(_fin_y_kernel, n_exp),
            grid=(tok // tm,),
            out_shape=[jax.ShapeDtypeStruct((tok, d_model), BF16), jax.ShapeDtypeStruct((tok, 128), BF16),
                       jax.ShapeDtypeStruct((d_model, 128), F32)],
            in_specs=[const_smem()] + [whole((rows_buf, d_model))] * 3 + [
                rows_spec(1), rows_spec(1), rows_spec(d_model), rows_spec(d_model), whole((d_model, 128))],
            out_specs=[rows_spec(d_model), rows_spec(128), whole((d_model, 128))],
            scratch_shapes=[pltpu.VMEM((rows_buf, d_model), BF16)],
            compiler_params=vm,
            cost_estimate=pl.CostEstimate(flops=8_000_000_000, bytes_accessed=20_000_000, transcendentals=0),
            name='fin_y',
        )(bounds, y_ret, y_0, y_dr, pos_col, idx_col, x, gy, wg_pad)
        grad_gate = lax.psum(dwg[:, :n_exp], ('dp', 'ep'))
        grad_x = pl.pallas_call(
            _fin_dx_kernel,
            grid=(tok // tm,),
            out_shape=jax.ShapeDtypeStruct((tok, d_model), BF16),
            in_specs=[const_smem()] + [whole((rows_buf, d_model))] * 3 + [
                rows_spec(1), rows_spec(128), whole((d_model, 128))],
            out_specs=rows_spec(d_model),
            scratch_shapes=[pltpu.VMEM((rows_buf, d_model), BF16)],
            compiler_params=vm,
            cost_estimate=pl.CostEstimate(flops=8_000_000_000, bytes_accessed=20_000_000, transcendentals=0),
            name='fin_dx',
        )(bounds, dx_ret, dx_0, dx_dr, pos_col, dz, wg_pad)
        return moe_out, grad_x, g1, g2, grad_gate

    return jax.shard_map(local_step, mesh=mesh,
                         in_specs=(tok_spec, tok_spec, idx_spec, rep_spec, exp_spec, exp_spec),
                         out_specs=(tok_spec, tok_spec, exp_spec, exp_spec, rep_spec), check_vma=False)
```

time: 1780 us -> 577 us (0.32)
  waiting for transfers between devices: 706 us -> 97.1 us
  matrix products: 364 us -> 0 us
  blocking collectives: 442 us -> 165 us
  Pallas kernels: 0 us -> 269 us
  local copies, waits for them, and re-layouts: 195 us -> 7.3 us
  other arithmetic: 36.8 us -> 7.5 us
    psum x1 -> x0, waiting for transfers between devices: 581 us -> none  [local_step(): grad_up = lax.psum(grad_up, 'dp')]
    dot_general x9 -> x0, matrix products: 364 us -> none  [the longest x1 98.3 us: local_step(): jnp.einsum('sekd,efd->eskf', recv_grad, w_down, preferred_element_type=jn...]
    all_to_all x2 -> x0, blocking collectives: 286 us -> none  [dispatch(): return lax.all_to_all(picked, 'ep', 0, 0, tiled=True)]
    pallas_call x0 -> x8, Pallas kernels: none -> 269 us  [the longest x4 207 us: _moe_call(): pl.pallas_call(functools.partial(_moe_kernel, cfg), out_shape=outs, in_sp...]
    gather x7 -> x0, local copies, waits for them, and re-layouts: 152 us -> none  [the longest x2 73.8 us: dispatch(): tok_rows[src_tok]]
    all_gather x0 -> x1, blocking collectives: none -> 130 us  [local_step(): meta_all = lax.all_gather(meta_loc, ('dp', 'ep'), axis=0, tiled=True)]
    all_to_all x2 -> x0, waiting for transfers between devices: 124 us -> none  [combine(): returned = lax.all_to_all(expert_rows, 'ep', 1, 0, tiled=True)]
    psum x1, blocking collectives: 156 us -> 35.1 us  [local_step(): grad_gate = lax.psum(dwg[:, :n_exp], ('dp', 'ep'))]
  transfers between devices with their start and end apart: 3 -> 20, of which waited for: 2 -> 2; matrix products, arithmetic and copies ran while one was open for 5% -> 3% of each run, Pallas kernels for 0% -> 42%
where the time goes in v1:
time: 577 us
  Pallas kernels  269 us (47%)
  blocking collectives  165 us (29%)
  waiting for transfers between devices  97.1 us (17%)
  starting transfers between devices  25.9 us (4%)
  other arithmetic  7.5 us (1%)
  local copies, waits for them, and re-layouts  7.3 us (1%)
    pallas_call x4, Pallas kernels, _moe_call(): pl.pallas_call(functools.partial(_moe_kernel, cfg), out_shape=outs, in_sp...  207 us
    all_gather x1, blocking collectives, local_step(): meta_all = lax.all_gather(meta_loc, ('dp', 'ep'), axis=0, tiled=True)  130 us
    ppermute x4, waiting for transfers between devices, cross_y(): return lax.ppermute(a, 'dp', [(i, 1 - i) for i in range(dp_size)])  97.1 us
    psum x1, blocking collectives, local_step(): grad_gate = lax.psum(dwg[:, :n_exp], ('dp', 'ep'))  35.1 us
    pallas_call x1, Pallas kernels, local_step(): pl.pallas_call(functools.partial(_fin_y_kernel, n_exp), grid=(tok // tm,)...  21.1 us
    ppermute x4, starting transfers between devices, cross_x(): return lax.ppermute(a, 'ep', [(i, i ^ 2) for i in range(ep_size)])  18.6 us
    pallas_call x1, Pallas kernels, local_step(): pl.pallas_call(_fin_dx_kernel, grid=(tok // tm,), out_shape=jax.ShapeDtyp...  16.3 us
    pallas_call x1, Pallas kernels, local_step(): pl.pallas_call(functools.partial(_sort_dy_kernel, n_exp), grid=(4,), out_...  13.9 us
  transfers between devices with their start and end apart: 20, of which 2 were waited for; matrix products, arithmetic and copies ran while one was open for 3% of the time, Pallas kernels for 42%

profile of v1, /device:TPU:0, one launch (start us, length us, event | category | flops | bytes accessed | tf_op | source)
XLA Modules:
  0.0 576.7 jit_solution(8900089074849070410)
XLA Ops:
  0.7 10.9 %sort_x.1 = (bf16[2176,768]{1,0:T(8,128)(2,1)}, s32[1,2048]{1,0:T(1,128)}, s32[16,128]{1,0:T(8,128)}) custom-call(s32[1,2048]{1,0:T(1,128)} %bitcast.12, bf16[2048,768]{1,0:T(8,128)(2,1)} %x_ref.5), custom_call_target="tpu_custom_call" | custom-call | flops 7000000000 | bytes 8000000 | tf_op jit(solution)/shard_map/sort_x/pallas_call | solution.py:457
  11.6 3.3 collective-permute-start
  14.9 1.3 copy.32.idxc_ref
  16.4 0.7 pad.4.wg_ref
  17.1 13.9 %sort_dy.1.refs_3_ = bf16[2176,768]{1,0:T(8,128)(2,1)} custom-call(s32[1,2048]{1,0:T(1,128)} %get-tuple-element.29.pos_ref, s32[2048,1]{1,0:T(8,128)} %copy.32.idxc_ref, bf16[2048,768]{1,0:T(8,128)(2,1)} %x_ref.5, bf16[2048,768]{1,0:T(8,128)(2,1)} %gy_ref.3, bf16[768,128]{1,0:T(8,128)(2,1)} %pad.4.wg_ref), custom_call_target="tpu_custom_call" | custom-call | flops 8000000000 | bytes 12000000 | tf_op jit(solution)/shard_map/sort_dy/pallas_call | solution.py:470
  31.6 2.0 collective-permute-start.16
  33.7 130.3 %all-gather = s32[8,1,16]{2,1,0:T(1,128)S(1)} all-gather(s32[1,1,16]{2,1,0:T(1,128)S(1)} %reshape.60), channel_id=1, replica_groups=mesh['dp'=2,'ep'=4] {'dp','ep'}, dimensions={0}, use_global_device_ids=true | all-gather | bytes 576 | tf_op jit(solution)/shard_map/all_gather | solution.py:484
  165.8 0.8 collective-permute-start.18
  166.7 1.2 collective-permute-start.12
  168.1 66.8 %shard_map.101 = (f32[2,768,3072]{2,1,0:T(8,128)}, f32[2,3072,768]{2,1,0:T(8,128)}, bf16[2176,768]{1,0:T(8,128)(2,1)}, bf16[2176,768]{1,0:T(8,128)(2,1)}, bf16[2...) custom-call(s32[128]{0:T(128)} %reshape.57.refs_0_, bf16[2176,768]{1,0:T(8,128)(2,1)} %get-tuple-element.28.refs_1_, ...), custom_call_target="tpu_custom_call" | custom-call | flops 44999999488 | bytes 60000000 | tf_op jit(solution)/shard_map/pallas_call | solution.py:367
  235.0 42.8 %shard_map.102 = (f32[2,768,3072]{2,1,0:T(8,128)}, f32[2,3072,768]{2,1,0:T(8,128)}, bf16[2176,768]{1,0:T(8,128)(2,1)}, bf16[2176,768]{1,0:T(8,128)(2,1)}, bf16[2...) custom-call(s32[128]{0:T(128)} %reshape.57.refs_0_, ...), custom_call_target="tpu_custom_call", output_to_operand_aliasing={{0}: (7, {}), {1}: (8, {})} | custom-call | flops 44999999488 | bytes 60000000 | tf_op jit(solution)/shard_map/pallas_call | solution.py:367
  277.8 0.9 collective-permute-start.9
  279.2 33.7 %collective-permute-done.12.refs_1_ = bf16[2176,768]{1,0:T(8,128)(2,1)} collective-permute-done((bf16[2176,768]{1,0:T(8,128)(2,1)}, bf16[2176,768]{1,0:T(8,128)(2,1)}, u32[]{:S(2)}, u32[]{:S(2)}) %collective-permute-start.12) | collective-permute-done | bytes 3342368 | tf_op jit(solution)/shard_map/ppermute | solution.py:494
  315.3 0.7 constant_dynamic-slice_fusion.1
  317.9 1.4 copy.33.posc_ref
  319.9 63.3 %collective-permute-done.14.refs_3_ = bf16[2176,768]{1,0:T(8,128)(2,1)} collective-permute-done((bf16[2176,768]{1,0:T(8,128)(2,1)}, bf16[2176,768]{1,0:T(8,128)(2,1)}, u32[]{:S(2)}, u32[]{:S(2)}) %collective-permute-start.14) | collective-permute-done | bytes 3342368 | tf_op jit(solution)/shard_map/ppermute | solution.py:494
  383.8 6.2 %broadcast_select_fusion = (bf16[2176,768]{1,0:T(8,128)(2,1)}, bf16[2176,768]{1,0:T(8,128)(2,1)}) fusion(bf16[2176,768]{1,0:T(8,128)(2,1)} %get-tuple-element.37, bf16[2176,768]{1,0:T(8,128)(2,1)S(1)} %collective-permute-done.9, pred[2176]{0:T(1024)(128)(4,1)S(1)} %fusion, bf16[2176,768]{1,0:T(8,128)(2,1)} %get-tuple-element.32, ...), kind=kLoop, calls=%fused_computation | loop fusion | flops 3342336 | bytes 20056192 | tf_op jit(solution)/shard_map/jit(_where)/select_n | solution.py:526
  390.8 42.3 %shard_map.103 = (f32[2,768,3072]{2,1,0:T(8,128)}, f32[2,3072,768]{2,1,0:T(8,128)}) custom-call(s32[128]{0:T(128)} %reshape.57.refs_0_, bf16[2176,768]{1,0:T(8,128)(2,1)} %collective-permute-done.16.refs_1_, bf16[2176,768]{1,0:T(8,128)(2,1)} %collective-permute-done.17.refs_2_, ...), custom_call_target="tpu_custom_call", output_to_operand_aliasing={{0}: (7, {}), {1}: (8, {})} | custom-call | flops 30000001024 | bytes 60000000 | tf_op jit(solution)/shard_map/pallas_call | solution.py:367
  433.1 15.0 %collective-permute-start.10 = (bf16[2176,768]{1,0:T(8,128)(2,1)}, bf16[2176,768]{1,0:T(8,128)(2,1)}, u32[]{:S(2)}, u32[]{:S(2)}) collective-permute-start(bf16[2176,768]{1,0:T(8,128)(2,1)} %get-tuple-element.67), channel_id=1, source_target_pairs={{0,2},{1,3},{2,0},{3,1},{4,6},{5,7},{6,4},{7,5}} | collective-permute-start | bytes 10027016 | tf_op jit(solution)/shard_map/ppermute | solution.py:491
  448.1 55.4 %shard_map.104 = (f32[2,768,3072]{2,1,0:T(8,128)}, f32[2,3072,768]{2,1,0:T(8,128)}) custom-call(s32[128]{0:T(128)} %reshape.57.refs_0_, bf16[2176,768]{1,0:T(8,128)(2,1)} %collective-permute-done.12.refs_1_, bf16[2176,768]{1,0:T(8,128)(2,1)} %collective-permute-done.13.refs_2_, ...), custom_call_target="tpu_custom_call", output_to_operand_aliasing={{0}: (7, {}), {1}: (8, {})} | custom-call | flops 30000001024 | bytes 60000000 | tf_op jit(solution)/shard_map/pallas_call | solution.py:367
  503.5 21.1 %fin_y.1 = (bf16[2048,768]{1,0:T(8,128)(2,1)}, bf16[2048,128]{1,0:T(8,128)(2,1)}, f32[768,128]{1,0:T(8,128)}) custom-call(s32[4]{0:T(128)} %compare_select_fusion.2.bounds, bf16[2176,768]{1,0:T(8,128)(2,1)} %collective-permute-done.7.far_ref, bf16[2176,768]{1,0:T(8,128)(2,1)} %get-tuple-element.34.mine_ref, ...), custom_call_target="tpu_custom_call" | custom-call | flops 8000000000 | bytes 20000000 | tf_op jit(solution)/shard_map/fin_y/pallas_call | solution.py:552
  524.6 35.1 %psum.7 = f32[768,8]{1,0:T(8,128)S(1)} all-reduce(f32[768,8]{1,0:T(8,128)} %bitcast.11), channel_id=1, replica_groups=mesh['dp'=2,'ep'=4] {'dp','ep'}, use_global_device_ids=true, to_apply=%region_0.1 | all-reduce | flops 6144 | bytes 49152 | tf_op jit(solution)/shard_map/psum | solution.py:565
  559.7 0.7 copy.36
  560.5 16.3 %fin_dx.1 = bf16[2048,768]{1,0:T(8,128)(2,1)} custom-call(s32[4]{0:T(128)} %compare_select_fusion.2.bounds, bf16[2176,768]{1,0:T(8,128)(2,1)} %collective-permute-done.10.far_ref, bf16[2176,768]{1,0:T(8,128)(2,1)} %get-tuple-element.39.mine_ref, bf16[2176,768]{1,0:T(8,128)(2,1)} %collective-permute-done.11.pair_ref, s32[2048,1]{1,0:T(8,128)} %copy.33.posc_ref, ...), custom_call_target="tpu_custom_call" | custom-call | flops 8000000000 | bytes 20000000 | tf_op jit(solution)/shard_map/fin_dx/pallas_call | solution.py:566
  (53 shorter events, 6.4 us)
Async XLA Ops:
  0.6 14.2 %copy-start.1 = (s32[2048]{0:T(1024)S(1)}, s32[2048]{0:T(1024)}, u32[]{:S(2)}) copy-start(s32[2048]{0:T(1024)} %param.8) | copy-start | bytes 24580
  0.6 15.6 %copy-start = (bf16[768,8]{0,1:T(8,128)(2,1)S(1)}, bf16[768,8]{0,1:T(8,128)(2,1)}, u32[]{:S(2)}) copy-start(bf16[768,8]{0,1:T(8,128)(2,1)} %param.9) | copy-start | bytes 36868
  11.6 154.3 %collective-permute-start = (bf16[2176,768]{1,0:T(8,128)(2,1)}, bf16[2176,768]{1,0:T(8,128)(2,1)}, u32[]{:S(2)}, u32[]{:S(2)}) collective-permute-start(bf16[2176,768]{1,0:T(8,128)(2,1)} %get-tuple-element.28.refs_1_), channel_id=1, source_target_pairs={{0,2},{1,3},{2,0},{3,1},{4,6},{5,7},{6,4},{7,5}} | collective-permute-start | bytes 10027016 | tf_op jit(solution)/shard_map/ppermute | solution.py:491
  17.1 16.5 %copy-start.3 = (s32[16,128]{1,0:T(8,128)S(1)}, s32[16,128]{1,0:T(8,128)}, u32[]{:S(2)}) copy-start(s32[16,128]{1,0:T(8,128)} %get-tuple-element.27) | copy-start | bytes 24580
  31.1 135.5 %collective-permute-start.2 = (bf16[2176,768]{1,0:T(8,128)(2,1)}, bf16[2176,768]{1,0:T(8,128)(2,1)}, u32[]{:S(2)}, u32[]{:S(2)}) collective-permute-start(bf16[2176,768]{1,0:T(8,128)(2,1)} %sort_dy.1.refs_3_), channel_id=1, source_target_pairs={{0,2},{1,3},{2,0},{3,1},{4,6},{5,7},{6,4},{7,5}} | collective-permute-start | bytes 10027016 | tf_op jit(solution)/shard_map/ppermute | solution.py:491
  31.1 135.6 %collective-permute-start.4 = (bf16[2176,768]{1,0:T(8,128)(2,1)}, bf16[2176,768]{1,0:T(8,128)(2,1)}, u32[]{:S(2)}, u32[]{:S(2)}) collective-permute-start(bf16[2176,768]{1,0:T(8,128)(2,1)} %get-tuple-element.28.refs_1_), channel_id=1, source_target_pairs={{0,1},{1,0},{2,3},{3,2},{4,5},{5,4},{6,7},{7,6}} | collective-permute-start | bytes 10027016 | tf_op jit(solution)/shard_map/ppermute | solution.py:488
  31.1 136.8 %collective-permute-start.5 = (bf16[2176,768]{1,0:T(8,128)(2,1)}, bf16[2176,768]{1,0:T(8,128)(2,1)}, u32[]{:S(2)}, u32[]{:S(2)}) collective-permute-start(bf16[2176,768]{1,0:T(8,128)(2,1)} %sort_dy.1.refs_3_), channel_id=1, source_target_pairs={{0,1},{1,0},{2,3},{3,2},{4,5},{5,4},{6,7},{7,6}} | collective-permute-start | bytes 10027016 | tf_op jit(solution)/shard_map/ppermute | solution.py:488
  31.6 247.1 %collective-permute-start.16 = (bf16[2176,768]{1,0:T(8,128)(2,1)}, bf16[2176,768]{1,0:T(8,128)(2,1)}, u32[]{:S(2)}, u32[]{:S(2)}) collective-permute-start(bf16[2176,768]{1,0:T(8,128)(2,1)} %get-tuple-element.28.refs_1_), channel_id=1, source_target_pairs={{0,4},{4,0},{1,5},{5,1},{2,6},{6,2},{3,7},{7,3}} | collective-permute-start | bytes 10027016 | tf_op jit(solution)/shard_map/ppermute | solution.py:494
  165.8 112.9 %collective-permute-start.18 = (bf16[2176,768]{1,0:T(8,128)(2,1)}, bf16[2176,768]{1,0:T(8,128)(2,1)}, u32[]{:S(2)}, u32[]{:S(2)}) collective-permute-start(bf16[2176,768]{1,0:T(8,128)(2,1)} %sort_dy.1.refs_3_), channel_id=1, source_target_pairs={{0,4},{4,0},{1,5},{5,1},{2,6},{6,2},{3,7},{7,3}} | collective-permute-start | bytes 10027016 | tf_op jit(solution)/shard_map/ppermute | solution.py:494
  166.6 68.3 %collective-permute-start.1 = (bf16[2176,768]{1,0:T(8,128)(2,1)}, bf16[2176,768]{1,0:T(8,128)(2,1)}, u32[]{:S(2)}, u32[]{:S(2)}) collective-permute-start(bf16[2176,768]{1,0:T(8,128)(2,1)} %collective-permute-done.refs_1_), channel_id=1, source_target_pairs={{0,1},{1,0},{2,3},{3,2},{4,5},{5,4},{6,7},{7,6}} | collective-permute-start | bytes 10027016 | tf_op jit(solution)/shard_map/ppermute | solution.py:488
  166.7 146.3 %collective-permute-start.12 = (bf16[2176,768]{1,0:T(8,128)(2,1)}, bf16[2176,768]{1,0:T(8,128)(2,1)}, u32[]{:S(2)}, u32[]{:S(2)}) collective-permute-start(bf16[2176,768]{1,0:T(8,128)(2,1)} %collective-permute-done.refs_1_), channel_id=1, source_target_pairs={{0,4},{4,0},{1,5},{5,1},{2,6},{6,2},{3,7},{7,3}} | collective-permute-start | bytes 10027016 | tf_op jit(solution)/shard_map/ppermute | solution.py:494
  167.9 67.1 %collective-permute-start.3 = (bf16[2176,768]{1,0:T(8,128)(2,1)}, bf16[2176,768]{1,0:T(8,128)(2,1)}, u32[]{:S(2)}, u32[]{:S(2)}) collective-permute-start(bf16[2176,768]{1,0:T(8,128)(2,1)} %collective-permute-done.2.refs_3_), channel_id=1, source_target_pairs={{0,1},{1,0},{2,3},{3,2},{4,5},{5,4},{6,7},{7,6}} | collective-permute-start | bytes 10027016 | tf_op jit(solution)/shard_map/ppermute | solution.py:488
  234.9 148.3 %collective-permute-start.14 = (bf16[2176,768]{1,0:T(8,128)(2,1)}, bf16[2176,768]{1,0:T(8,128)(2,1)}, u32[]{:S(2)}, u32[]{:S(2)}) collective-permute-start(bf16[2176,768]{1,0:T(8,128)(2,1)} %collective-permute-done.2.refs_3_), channel_id=1, source_target_pairs={{0,4},{4,0},{1,5},{5,1},{2,6},{6,2},{3,7},{7,3}} | collective-permute-start | bytes 10027016 | tf_op jit(solution)/shard_map/ppermute | solution.py:494
  235.0 82.9 %copy-start.2 = (s32[1,2048]{1,0:T(1,128)S(1)}, s32[1,2048]{1,0:T(1,128)}, u32[]{:S(2)}) copy-start(s32[1,2048]{1,0:T(1,128)} %get-tuple-element.29.pos_ref) | copy-start | bytes 24580
  277.8 105.4 %collective-permute-start.9 = (bf16[2176,768]{1,0:T(8,128)(2,1)}, bf16[2176,768]{1,0:T(8,128)(2,1)S(1)}, u32[]{:S(2)}, u32[]{:S(2)}) collective-permute-start(bf16[2176,768]{1,0:T(8,128)(2,1)} %get-tuple-element.38), channel_id=1, source_target_pairs={{0,1},{1,0},{2,3},{3,2},{4,5},{5,4},{6,7},{7,6}} | collective-permute-start | bytes 10027016 | tf_op jit(solution)/shard_map/ppermute | solution.py:488
  278.7 105.0 %collective-permute-start.6 = (bf16[2176,768]{1,0:T(8,128)(2,1)}, bf16[2176,768]{1,0:T(8,128)(2,1)}, u32[]{:S(2)}, u32[]{:S(2)}) collective-permute-start(bf16[2176,768]{1,0:T(8,128)(2,1)} %get-tuple-element.33), channel_id=1, source_target_pairs={{0,1},{1,0},{2,3},{3,2},{4,5},{5,4},{6,7},{7,6}} | collective-permute-start | bytes 10027016 | tf_op jit(solution)/shard_map/ppermute | solution.py:488
  278.8 111.2 %collective-permute-start.17 = (bf16[2176,768]{1,0:T(8,128)(2,1)}, bf16[2176,768]{1,0:T(8,128)(2,1)}, u32[]{:S(2)}, u32[]{:S(2)}) collective-permute-start(bf16[2176,768]{1,0:T(8,128)(2,1)} %collective-permute-done.16.refs_1_), channel_id=1, source_target_pairs={{0,1},{1,0},{2,3},{3,2},{4,5},{5,4},{6,7},{7,6}} | collective-permute-start | bytes 10027016 | tf_op jit(solution)/shard_map/ppermute | solution.py:488
  313.0 77.5 %collective-permute-start.19 = (bf16[2176,768]{1,0:T(8,128)(2,1)}, bf16[2176,768]{1,0:T(8,128)(2,1)}, u32[]{:S(2)}, u32[]{:S(2)}) collective-permute-start(bf16[2176,768]{1,0:T(8,128)(2,1)} %collective-permute-done.18.refs_3_), channel_id=1, source_target_pairs={{0,1},{1,0},{2,3},{3,2},{4,5},{5,4},{6,7},{7,6}} | collective-permute-start | bytes 10027016 | tf_op jit(solution)/shard_map/ppermute | solution.py:488
  383.2 120.3 %collective-permute-start.8 = (bf16[2176,768]{1,0:T(8,128)(2,1)}, bf16[2176,768]{1,0:T(8,128)(2,1)}, u32[]{:S(2)}, u32[]{:S(2)}) collective-permute-start(bf16[2176,768]{1,0:T(8,128)(2,1)} %get-tuple-element.35), channel_id=1, source_target_pairs={{0,1},{1,0},{2,3},{3,2},{4,5},{5,4},{6,7},{7,6}} | collective-permute-start | bytes 10027016 | tf_op jit(solution)/shard_map/ppermute | solution.py:488
  383.2 49.9 %collective-permute-start.13 = (bf16[2176,768]{1,0:T(8,128)(2,1)}, bf16[2176,768]{1,0:T(8,128)(2,1)}, u32[]{:S(2)}, u32[]{:S(2)}) collective-permute-start(bf16[2176,768]{1,0:T(8,128)(2,1)} %collective-permute-done.12.refs_1_), channel_id=1, source_target_pairs={{0,1},{1,0},{2,3},{3,2},{4,5},{5,4},{6,7},{7,6}} | collective-permute-start | bytes 10027016 | tf_op jit(solution)/shard_map/ppermute | solution.py:488
  383.7 64.3 %collective-permute-start.15 = (bf16[2176,768]{1,0:T(8,128)(2,1)}, bf16[2176,768]{1,0:T(8,128)(2,1)}, u32[]{:S(2)}, u32[]{:S(2)}) collective-permute-start(bf16[2176,768]{1,0:T(8,128)(2,1)} %collective-permute-done.14.refs_3_), channel_id=1, source_target_pairs={{0,1},{1,0},{2,3},{3,2},{4,5},{5,4},{6,7},{7,6}} | collective-permute-start | bytes 10027016 | tf_op jit(solution)/shard_map/ppermute | solution.py:488
  390.0 170.5 %collective-permute-start.11 = (bf16[2176,768]{1,0:T(8,128)(2,1)}, bf16[2176,768]{1,0:T(8,128)(2,1)}, u32[]{:S(2)}, u32[]{:S(2)}) collective-permute-start(bf16[2176,768]{1,0:T(8,128)(2,1)} %get-tuple-element.40), channel_id=1, source_target_pairs={{0,1},{1,0},{2,3},{3,2},{4,5},{5,4},{6,7},{7,6}} | collective-permute-start | bytes 10027016 | tf_op jit(solution)/shard_map/ppermute | solution.py:488
  390.5 113.0 %collective-permute-start.7 = (bf16[2176,768]{1,0:T(8,128)(2,1)}, bf16[2176,768]{1,0:T(8,128)(2,1)}, u32[]{:S(2)}, u32[]{:S(2)}) collective-permute-start(bf16[2176,768]{1,0:T(8,128)(2,1)} %get-tuple-element.68), channel_id=1, source_target_pairs={{0,2},{1,3},{2,0},{3,1},{4,6},{5,7},{6,4},{7,5}} | collective-permute-start | bytes 10027016 | tf_op jit(solution)/shard_map/ppermute | solution.py:491
  433.1 127.4 %collective-permute-start.10 = (bf16[2176,768]{1,0:T(8,128)(2,1)}, bf16[2176,768]{1,0:T(8,128)(2,1)}, u32[]{:S(2)}, u32[]{:S(2)}) collective-permute-start(bf16[2176,768]{1,0:T(8,128)(2,1)} %get-tuple-element.67), channel_id=1, source_target_pairs={{0,2},{1,3},{2,0},{3,1},{4,6},{5,7},{6,4},{7,5}} | collective-permute-start | bytes 10027016 | tf_op jit(solution)/shard_map/ppermute | solution.py:491
